TPU v7x, 32 devices: a whole 2x2x4 slice. The times are simulated.
32 devices in a mesh: dp: 4 (over y, core), tensor: 8 (over z, x).
Axes of the slice: x: 2, y: 2, z: 4, core: 2. Of those that a mesh axis runs over, the one named last changes fastest.
Arguments:
- ref_hidden: bfloat16 [1152, 4608], P('dp', 'tensor'), may hold values from -6 to 6
- pol_hidden: bfloat16 [1152, 4608], P('dp', 'tensor'), may hold values from -6 to 6
- readout: bfloat16 [1152, 4608], P('dp', 'tensor'), may hold values from -0.019897461 to 0.019897461
- lengths: int32 [12], P('dp'), may hold values from 16 to 96, as said below
- pairing: int32 [12], replicated, may hold values from 0 to 11, each once
- pre_gain: float32 [4608], replicated, may hold values from 0.25 to 1.75
- post_gain: float32 [4608], replicated, may hold values from 0.25 to 1.75
- w_query: bfloat16 [4608, 4096], P('dp', 'tensor'), may hold values from -0.09375 to 0.09375
- w_key: bfloat16 [4608, 2048], P('dp', 'tensor'), may hold values from -3 to 3
- value_projection: bfloat16 [4608, 2048], P('dp', 'tensor'), may hold values from -0.09375 to 0.09375
- w_out: bfloat16 [4608, 4096], P('dp', 'tensor'), may hold values from -0.09375 to 0.09375
- a_query: bfloat16 [4608, 64], P('dp'), may hold values from -0.09375 to 0.09375
- a_value: bfloat16 [4608, 64], P('dp'), may hold values from -0.09375 to 0.09375
- query_second_factor: bfloat16 [64, 4096], P(None, 'tensor'), may hold values from -0.75 to 0.75
- value_second_factor: bfloat16 [64, 2048], P(None, 'tensor'), may hold values from -0.75 to 0.75
Outputs:
- policy_out: bfloat16 [1152, 4608], P('dp', 'tensor')
- reference_out: bfloat16 [1152, 4608], P('dp', 'tensor')
- dpo_loss: float32 [], replicated
- grad_hidden: bfloat16 [1152, 4608], P('dp', 'tensor')
- grad_a: float32 [4608, 128], P('dp')
- query_factor_gradient: float32 [64, 4096], P(None, 'tensor')
- value_factor_gradient: float32 [64, 2048], P(None, 'tensor')
Inputs may be any that keep to these rules, and one draw needn't show every extreme that they name: `lengths`: every sequence has at least one valid token and some sequence is full. `pairing`: entries 2k and 2k + 1 name the chosen and the rejected sequence of pair k; every sequence appears once.
All inputs are finite; a program needn't handle non-finite values.
Results may differ from a plain program's by a relative error of at most 0.0233.
The roundings to bfloat16 on the way count: a program that leaves them out, or rounds other values in their place, can miss the bound.
Values may be sent and summed in bfloat16 or wider, within the bound.
A program may use at most 128 MiB of HBM per device.

v0:
```python
import jax
import jax.numpy as jnp
from jax import lax
from jax.sharding import PartitionSpec as P

MODEL_WIDTH = 4608
HQ = 32
HEAD_SIZE = 128
NORM_EPS = 1e-06
SOFT_CAP = 50.0
ADAPTER_SCALE = 0.5
DPO_BETA = 0.5
LOSS_SCALE = 256.0
ROPE_BASE = 10000.0


def query_scale():
    return float(MODEL_WIDTH // HQ) ** (-0.5)


def apply_rotation(value_rows, direction):
    length = value_rows.shape[1]
    head_depth = value_rows.shape[3]
    middle = head_depth // 2
    spacing = ROPE_BASE ** (-2.0 * jnp.arange(middle, dtype=jnp.float32) / head_depth)
    angles = jnp.arange(length, dtype=jnp.float32)[:, None] * spacing[None, :]
    cosine = jnp.cos(angles)[None, :, None, :]
    sine_part = direction * jnp.sin(angles)[None, :, None, :]
    leading = value_rows[..., :middle]
    trailing = value_rows[..., middle:]
    return jnp.concatenate(
        [leading * cosine - trailing * sine_part, trailing * cosine + leading * sine_part], axis=-1
    )


def allowed_mask(lengths, length):
    places = jnp.arange(length)
    causal = places[None, :] <= places[:, None]
    living = places[None, :] < lengths[:, None]
    return causal[None, None, None, :, :] & living[:, None, None, None, :]


def attend(query_rows, rotated_keys, value_rows, lengths):
    seqs_here, length, q_heads, head_depth = query_rows.shape
    kv_heads = rotated_keys.shape[2]
    grouped_heads = query_rows.reshape(seqs_here, length, kv_heads, q_heads // kv_heads, head_depth)
    scores = (
        jnp.einsum(
            "sqkgd,spkd->skgqp", grouped_heads, rotated_keys, preferred_element_type=jnp.float32
        )
        * query_scale()
    )
    capped = SOFT_CAP * jnp.tanh(scores / SOFT_CAP)
    allowed = allowed_mask(lengths, length)
    weights = jnp.where(allowed, jnp.exp(capped), 0.0)
    probabilities = weights / jnp.sum(weights, axis=-1, keepdims=True)
    probs_low = probabilities.astype(jnp.bfloat16)
    mixed_out = jnp.einsum(
        "skgqp,spkd->sqkgd", probs_low, value_rows, preferred_element_type=jnp.float32
    )
    return (
        mixed_out.astype(jnp.bfloat16).reshape(seqs_here, length, q_heads, head_depth),
        probs_low,
        probabilities,
        capped,
    )


def attend_back(grad_mixed, query_rows, rotated_keys, value_rows, probs_low, probabilities, capped):
    seqs_here, length, q_heads, head_depth = query_rows.shape
    kv_heads = rotated_keys.shape[2]
    shape_five = (seqs_here, length, kv_heads, q_heads // kv_heads, head_depth)
    grouped_heads = query_rows.reshape(shape_five)
    grad_grouped = grad_mixed.reshape(shape_five)
    grad_probs = jnp.einsum(
        "sqkgd,spkd->skgqp", grad_grouped, value_rows, preferred_element_type=jnp.float32
    )
    value_rows_gradient = jnp.einsum(
        "skgqp,sqkgd->spkd", probs_low, grad_grouped, preferred_element_type=jnp.float32
    )
    centered = grad_probs - jnp.sum(grad_probs * probabilities, axis=-1, keepdims=True)
    grad_scores = (
        probabilities * centered * (1.0 - (capped / SOFT_CAP) ** 2) * query_scale()
    ).astype(jnp.bfloat16)
    query_rows_gradient = jnp.einsum(
        "skgqp,spkd->sqkgd", grad_scores, rotated_keys, preferred_element_type=jnp.float32
    ).reshape(seqs_here, length, q_heads, head_depth)
    key_rows_gradient = jnp.einsum(
        "skgqp,sqkgd->spkd", grad_scores, grouped_heads, preferred_element_type=jnp.float32
    )
    return (query_rows_gradient, key_rows_gradient, value_rows_gradient)


def normalize(hidden, pre_gain):
    whole_rows = lax.all_gather(hidden, "tensor", axis=1, tiled=True)
    wide_rows = whole_rows.astype(jnp.float32)
    pre_scale = lax.rsqrt(
        jnp.sum(wide_rows * wide_rows, axis=1, keepdims=True) / pre_gain.shape[0] + NORM_EPS
    )
    normed = (wide_rows * pre_scale * pre_gain).astype(jnp.bfloat16)
    return (normed, pre_scale)


def attention_layer(hidden, normed, weights, adapters, lengths, post_local):
    w_query, w_key, value_projection, w_out, a_query, a_value = weights
    tok_rows, full_width = normed.shape
    seqs_here = lengths.shape[0]
    length = tok_rows // seqs_here
    query_rows = jnp.dot(normed, w_query, preferred_element_type=jnp.float32)
    keys_before_rotation = jnp.dot(normed, w_key, preferred_element_type=jnp.float32)
    value_rows = jnp.dot(normed, value_projection, preferred_element_type=jnp.float32)
    low_rank_update = None
    if adapters is not None:
        query_second_factor, value_second_factor = adapters
        rank_size = query_second_factor.shape[0]
        low_rank_update = jnp.dot(
            normed, jnp.concatenate([a_query, a_value], axis=1), preferred_element_type=jnp.float32
        ).astype(jnp.bfloat16)
        query_rows = query_rows + ADAPTER_SCALE * jnp.dot(
            low_rank_update[:, :rank_size], query_second_factor, preferred_element_type=jnp.float32
        )
        value_rows = value_rows + ADAPTER_SCALE * jnp.dot(
            low_rank_update[:, rank_size:], value_second_factor, preferred_element_type=jnp.float32
        )
    q_heads = query_rows.shape[1] // HEAD_SIZE
    kv_heads = keys_before_rotation.shape[1] // HEAD_SIZE
    query_rows = apply_rotation(
        query_rows.reshape(seqs_here, length, q_heads, HEAD_SIZE), 1.0
    ).astype(jnp.bfloat16)
    rotated_keys = apply_rotation(
        keys_before_rotation.reshape(seqs_here, length, kv_heads, HEAD_SIZE), 1.0
    ).astype(jnp.bfloat16)
    value_rows = value_rows.reshape(seqs_here, length, kv_heads, HEAD_SIZE).astype(jnp.bfloat16)
    mixed_out, probs_low, probabilities, capped = attend(
        query_rows, rotated_keys, value_rows, lengths
    )
    head_terms = lax.dot_general(
        mixed_out.reshape(tok_rows, q_heads * HEAD_SIZE),
        w_out,
        (((1,), (1,)), ((), ())),
        preferred_element_type=jnp.float32,
    )
    summed = lax.psum_scatter(
        head_terms.astype(jnp.bfloat16), "tensor", scatter_dimension=1, tiled=True
    ).astype(jnp.float32)
    squares = lax.psum(jnp.sum(summed * summed, axis=1), "tensor")
    post_scale = lax.rsqrt(squares[:, None] / full_width + NORM_EPS)
    result = hidden.astype(jnp.float32) + summed * post_scale * post_local
    saved = (
        low_rank_update,
        query_rows,
        rotated_keys,
        value_rows,
        probs_low,
        probabilities,
        capped,
        summed,
        post_scale,
    )
    return (result, saved)


def body(
    ref_hidden,
    pol_hidden,
    readout,
    lengths,
    pairing,
    pre_gain,
    post_gain,
    w_query,
    w_key,
    value_projection,
    w_out,
    a_query,
    a_value,
    query_second_factor,
    value_second_factor,
):
    tok_rows, part_width = pol_hidden.shape
    seqs_here = lengths.shape[0]
    length = tok_rows // seqs_here
    tensor_rank = lax.axis_index("tensor")
    data_rank = lax.axis_index("dp")
    all_seqs = seqs_here * lax.axis_size("dp")
    full_width = part_width * lax.axis_size("tensor")
    pre_local = lax.dynamic_slice_in_dim(pre_gain, tensor_rank * part_width, part_width)
    post_local = lax.dynamic_slice_in_dim(post_gain, tensor_rank * part_width, part_width)
    weights = (
        lax.all_gather(w_query, "dp", axis=0, tiled=True),
        lax.all_gather(w_key, "dp", axis=0, tiled=True),
        lax.all_gather(value_projection, "dp", axis=0, tiled=True),
        lax.all_gather(w_out, "dp", axis=0, tiled=True),
        lax.all_gather(a_query, "dp", axis=0, tiled=True),
        lax.all_gather(a_value, "dp", axis=0, tiled=True),
    )
    w_query_all, w_key_all, w_value_all, w_out_all, a_query_all, a_value_all = weights
    ref_normed, ref_scale = normalize(ref_hidden, pre_gain)
    ref_result, ref_saved = attention_layer(
        ref_hidden, ref_normed, weights, None, lengths, post_local
    )
    pol_normed, pol_scale = normalize(pol_hidden, pre_gain)
    pol_result, pol_saved = attention_layer(
        pol_hidden,
        pol_normed,
        weights,
        (query_second_factor, value_second_factor),
        lengths,
        post_local,
    )
    readout_wide = readout.astype(jnp.float32)
    living = (jnp.arange(length)[None, :] < lengths[:, None]).astype(jnp.float32)

    def sequence_score(result):
        return jnp.sum(
            jnp.sum(result * readout_wide, axis=1).reshape(seqs_here, length) * living, axis=1
        )

    placed = jnp.zeros((2, all_seqs), jnp.float32)
    offset = data_rank * seqs_here
    placed = lax.dynamic_update_slice(
        placed,
        jnp.stack([sequence_score(ref_result), sequence_score(pol_result)]),
        (jnp.int32(0), offset),
    )
    scores = lax.psum(placed, ("dp", "tensor"))
    ratios = scores[1] - scores[0]
    chooser = (pairing[:, None] == jnp.arange(all_seqs)[None, :]).astype(jnp.float32)
    picked = jnp.dot(chooser, ratios, precision=lax.Precision.HIGHEST).reshape(-1, 2)
    margins = DPO_BETA * (picked[:, 0] - picked[:, 1])
    dpo_loss = jnp.sum(jax.nn.softplus(-margins))
    pair_pull = DPO_BETA * LOSS_SCALE * jax.nn.sigmoid(-margins)
    signed = jnp.stack([-pair_pull, pair_pull], axis=1).reshape(-1)
    coefficients = jnp.dot(signed, chooser, precision=lax.Precision.HIGHEST)
    local_coef = lax.dynamic_slice_in_dim(coefficients, offset, seqs_here)
    grad_result = (local_coef[:, None] * living).reshape(tok_rows, 1) * readout_wide
    (
        low_rank_update,
        query_rows,
        rotated_keys,
        value_rows,
        probs_low,
        probabilities,
        capped,
        summed,
        post_scale,
    ) = pol_saved
    post_dot = lax.psum(jnp.sum(summed * post_local * grad_result, axis=1), "tensor")
    grad_summed = (
        post_scale * post_local * grad_result
        - summed * post_scale**3 * post_dot[:, None] / full_width
    )
    grad_wide = lax.all_gather(grad_summed.astype(jnp.bfloat16), "tensor", axis=1, tiled=True)
    grad_mixed = jnp.dot(grad_wide, w_out_all, preferred_element_type=jnp.float32).astype(
        jnp.bfloat16
    )
    q_heads = query_rows.shape[2]
    grad_q_rot, rotated_key_gradient, value_head_gradient = attend_back(
        grad_mixed.reshape(seqs_here, length, q_heads, HEAD_SIZE),
        query_rows,
        rotated_keys,
        value_rows,
        probs_low,
        probabilities,
        capped,
    )
    query_rows_gradient = (
        apply_rotation(grad_q_rot, -1.0).reshape(tok_rows, -1).astype(jnp.bfloat16)
    )
    key_rows_gradient = (
        apply_rotation(rotated_key_gradient, -1.0).reshape(tok_rows, -1).astype(jnp.bfloat16)
    )
    value_rows_gradient = value_head_gradient.reshape(tok_rows, -1).astype(jnp.bfloat16)
    rank_size = query_second_factor.shape[0]
    rows_contraction = (((0,), (0,)), ((), ()))
    contract_cols = (((1,), (1,)), ((), ()))
    query_adapter_term = ADAPTER_SCALE * lax.dot_general(
        low_rank_update[:, :rank_size],
        query_rows_gradient,
        rows_contraction,
        preferred_element_type=jnp.float32,
    )
    value_adapter_term = ADAPTER_SCALE * lax.dot_general(
        low_rank_update[:, rank_size:],
        value_rows_gradient,
        rows_contraction,
        preferred_element_type=jnp.float32,
    )
    query_factor_gradient, value_factor_gradient = (
        lax.psum(query_adapter_term.astype(jnp.bfloat16), "dp").astype(jnp.float32),
        lax.psum(value_adapter_term.astype(jnp.bfloat16), "dp").astype(jnp.float32),
    )
    adapter_grad = jnp.concatenate(
        [
            ADAPTER_SCALE
            * lax.dot_general(
                query_rows_gradient,
                query_second_factor,
                contract_cols,
                preferred_element_type=jnp.float32,
            ),
            ADAPTER_SCALE
            * lax.dot_general(
                value_rows_gradient,
                value_second_factor,
                contract_cols,
                preferred_element_type=jnp.float32,
            ),
        ],
        axis=1,
    ).astype(jnp.bfloat16)
    adapter_term = lax.dot_general(
        pol_normed, adapter_grad, rows_contraction, preferred_element_type=jnp.float32
    )
    adapter_part = lax.psum_scatter(
        adapter_term.astype(jnp.bfloat16), "dp", scatter_dimension=0, tiled=True
    )
    grad_a = lax.psum(adapter_part, "tensor").astype(jnp.float32)
    a_both = jnp.concatenate([a_query_all, a_value_all], axis=1)
    input_terms = lax.dot_general(
        query_rows_gradient, w_query_all, contract_cols, preferred_element_type=jnp.float32
    )
    input_terms = input_terms + lax.dot_general(
        key_rows_gradient, w_key_all, contract_cols, preferred_element_type=jnp.float32
    )
    input_terms = input_terms + lax.dot_general(
        value_rows_gradient, w_value_all, contract_cols, preferred_element_type=jnp.float32
    )
    input_terms = input_terms + lax.dot_general(
        adapter_grad, a_both, contract_cols, preferred_element_type=jnp.float32
    )
    input_whole = lax.psum(input_terms.astype(jnp.bfloat16), "tensor").astype(jnp.float32)
    grad_normed = lax.dynamic_slice_in_dim(input_whole, tensor_rank * part_width, part_width, 1)
    narrow = pol_hidden.astype(jnp.float32)
    pre_dot = lax.psum(jnp.sum(narrow * pre_local * grad_normed, axis=1), "tensor")
    grad_hidden = (
        grad_result
        + pol_scale * pre_local * grad_normed
        - narrow * pol_scale**3 * pre_dot[:, None] / full_width
    )
    return (
        pol_result.astype(jnp.bfloat16),
        ref_result.astype(jnp.bfloat16),
        dpo_loss,
        grad_hidden.astype(jnp.bfloat16),
        grad_a,
        query_factor_gradient,
        value_factor_gradient,
    )


def solution(mesh):
    placed = (
        P("dp", "tensor"),
        P("dp", "tensor"),
        P("dp", "tensor"),
        P("dp"),
        P(),
        P(),
        P(),
        P("dp", "tensor"),
        P("dp", "tensor"),
        P("dp", "tensor"),
        P("dp", "tensor"),
        P("dp", None),
        P("dp", None),
        P(None, "tensor"),
        P(None, "tensor"),
    )
    return jax.shard_map(
        body,
        mesh=mesh,
        in_specs=placed,
        out_specs=(
            P("dp", "tensor"),
            P("dp", "tensor"),
            P(),
            P("dp", "tensor"),
            P("dp", None),
            P(None, "tensor"),
            P(None, "tensor"),
        ),
        check_vma=False,
    )
```

profile of v0, /device:TPU:0, one launch (start us, length us, event | category | flops | bytes accessed | tf_op | source)
XLA Modules:
  0.0 823.5 jit_solution(8016594998505936199)
XLA Ops:
  11.2 9.0 %all_gather.29 = bf16[4608,64]{0,1:T(8,128)(2,1)S(1)} all-gather(bf16[1152,64]{0,1:T(8,128)(2,1)S(1)} %copy-done.29), channel_id=1, replica_groups=mesh['dp'=4,'tensor'=8] {'dp'}, dimensions={0}, use_global_device_ids=true | all-gather | bytes 737280 | tf_op jit(solution)/shard_map/all_gather | solution.py:194
  20.3 7.6 all_gather.30
  29.8 41.2 %all-gather.21.cloned.1.call-done = bf16[8,576,288]{1,2,0:T(8,128)(2,1)} async-done(((bf16[1,576,288]{1,2,0:T(8,128)(2,1)}), bf16[8,576,288]{1,2,0:T(8,128)(2,1)}) %all-gather.21.cloned.1.call-update) | async-done | bytes 2654224 | tf_op jit(solution)/shard_map/all_gather | solution.py:95
  71.0 5.3 copy.72
  76.4 7.2 reshape.270
  83.6 46.3 %all-gather.19.cloned.1.call-done = bf16[8,576,288]{1,2,0:T(8,128)(2,1)} async-done(((bf16[1,576,288]{1,2,0:T(8,128)(2,1)}), bf16[8,576,288]{1,2,0:T(8,128)(2,1)}) %all-gather.19.cloned.1.call-update) | async-done | bytes 2654224 | tf_op jit(solution)/shard_map/all_gather | solution.py:95
  129.8 5.3 copy.64
  135.2 7.8 reshape.269
  143.0 3.1 multiply_reduce_fusion
  149.6 3.3 multiply_convert_fusion
  154.1 3.3 fusion.141
  157.6 3.2 fusion.139
  162.0 17.6 %all-gather.11.cloned.1.call-done = bf16[4608,256]{1,0:T(8,128)(2,1)} async-done(((bf16[1152,256]{1,0:T(8,128)(2,1)}), bf16[4608,256]{1,0:T(8,128)(2,1)}) %all-gather.11.cloned.1.call-update) | async-done | bytes 2359312 | tf_op jit(solution)/shard_map/all_gather | solution.py:192
  179.6 3.3 convolution_convert_fusion.6
  186.1 32.4 %all-gather.15.cloned.1.call-done = bf16[4608,512]{1,0:T(8,128)(2,1)} async-done(((bf16[1152,512]{1,0:T(8,128)(2,1)}), bf16[4608,512]{1,0:T(8,128)(2,1)}) %all-gather.15.cloned.1.call-update) | async-done | bytes 4718608 | tf_op jit(solution)/shard_map/all_gather | solution.py:190
  218.5 5.5 fusion.142
  225.2 4.4 fusion.140
  230.7 2.1 reshape.256
  232.8 2.9 subtract_convert_fusion.1
  239.0 18.4 %all-gather.17.cloned.1.call-done = bf16[4608,512]{1,0:T(8,128)(2,1)} async-done(((bf16[1152,512]{1,0:T(8,128)(2,1)}), bf16[4608,512]{1,0:T(8,128)(2,1)}) %all-gather.17.cloned.1.call-update) | async-done | bytes 4718608 | tf_op jit(solution)/shard_map/all_gather | solution.py:193
  257.4 5.4 convolution_convert_fusion
  262.8 4.7 copy.110
  267.8 2.5 fusion.138
  276.2 5.6 convolution_convert_fusion.1
  281.8 4.7 copy.108
  288.0 59.2 %reduce-scatter.12.cloned.1.call-done = bf16[576,288]{1,0:T(8,128)(2,1)} async-done(((bf16[4608,288]{1,0:T(8,128)(2,1)}), bf16[576,288]{1,0:T(8,128)(2,1)}) %reduce-scatter.12.cloned.1.call-update) | async-done | bytes 331792
  349.1 80.8 %reduce-scatter.10.cloned.1.call-done = bf16[576,288]{1,0:T(8,128)(2,1)} async-done(((bf16[4608,288]{1,0:T(8,128)(2,1)}), bf16[576,288]{1,0:T(8,128)(2,1)}) %reduce-scatter.10.cloned.1.call-update) | async-done | bytes 331792
  432.4 20.1 %all-reduce = (f32[288]{0:T(512)S(1)}, f32[288]{0:T(512)S(1)}) all-reduce(f32[288]{0:T(512)S(1)} %fusion.45, f32[288]{0:T(512)S(1)} %fusion.32), channel_id=1, replica_groups=mesh['dp'=4,'tensor'=8] {'tensor'}, use_global_device_ids=true, to_apply=%region_4.5 | all-reduce | flops 576 | bytes 4608 | tf_op jit(solution)/shard_map/psum | solution.py:146
  452.5 2.6 fusion.43
  457.0 36.8 %psum.65 = f32[2,12]{1,0:T(2,128)S(1)} all-reduce(f32[2,12]{1,0:T(2,128)S(1)} %dynamic_update_slice.3), channel_id=1, replica_groups=mesh['dp'=4,'tensor'=8] {'dp','tensor'}, use_global_device_ids=true, to_apply=%region_14.15 | all-reduce | flops 24 | bytes 192 | tf_op jit(solution)/shard_map/psum | solution.py:226
  496.8 21.1 %psum.66 = f32[288]{0:T(512)S(1)} all-reduce(f32[288]{0:T(512)S(1)} %fusion.38), channel_id=1, replica_groups=mesh['dp'=4,'tensor'=8] {'tensor'}, use_global_device_ids=true, to_apply=%region_17.18 | all-reduce | flops 288 | bytes 2304 | tf_op jit(solution)/shard_map/psum | solution.py:248
  519.2 55.1 %all-gather.23.cloned.1.call-done = bf16[8,576,288]{1,2,0:T(8,128)(2,1)} async-done(((bf16[1,576,288]{1,2,0:T(8,128)(2,1)}), bf16[8,576,288]{1,2,0:T(8,128)(2,1)}) %all-gather.23.cloned.1.call-update) | async-done | bytes 2654224 | tf_op jit(solution)/shard_map/all_gather | solution.py:253
  574.4 4.4 copy.82
  578.8 5.6 reshape.268
  584.4 5.4 convolution_convert_fusion.3
  590.9 2.1 convolution_bitcast_fusion
  592.9 2.0 fusion.19
  595.0 3.3 fusion.27
  602.9 2.2 convolution_convert_fusion.2
  605.2 2.5 convolution_bitcast_fusion.2
  609.0 4.3 fusion.58
  616.3 2.4 fusion.1
  618.7 10.8 %reduce-scatter.8.cloned.1.call-done = bf16[1152,128]{1,0:T(8,128)(2,1)} async-done(((bf16[4608,128]{1,0:T(8,128)(2,1)}), bf16[1152,128]{1,0:T(8,128)(2,1)}) %reduce-scatter.8.cloned.1.call-update) | async-done | bytes 294928 | tf_op jit(solution)/shard_map/reduce_scatter | solution.py:315
  631.2 10.5 %psum.71 = bf16[64,256]{1,0:T(8,128)(2,1)S(1)} all-reduce(bf16[64,256]{1,0:T(8,128)(2,1)S(1)} %fusion.23), channel_id=1, replica_groups=mesh['dp'=4,'tensor'=8] {'dp'}, use_global_device_ids=true, to_apply=%region_25.26 | all-reduce | flops 16384 | bytes 65536 | tf_op jit(solution)/shard_map/psum | solution.py:291
  642.4 21.6 %all-reduce.5.cloned.1.call-done = bf16[64,512]{1,0:T(8,128)(2,1)} async-done(((bf16[64,512]{1,0:T(8,128)(2,1)}), bf16[64,512]{1,0:T(8,128)(2,1)}) %all-reduce.5.cloned.1.call-update) | async-done | bytes 65552 | tf_op jit(solution)/shard_map/psum | solution.py:290
  665.5 126.0 %all-reduce.7.cloned.1.call-done = (bf16[288,4608]{1,0:T(8,128)(2,1)}, bf16[1152,128]{1,0:T(8,128)(2,1)}) async-done(((bf16[288,4608]{1,0:T(8,128)(2,1)}, bf16[1152,128]{1,0:T(8,128)(2,1)}), (bf16[288,4608]{1,0:T(8,128)(2,1)}, bf16[1152,128]{1,0:T(8,128)(2,1)})) %all-reduce.7.cloned.1.call-update) | async-done | bytes 2949136 | tf_op jit(solution)/shard_map/psum | solution.py:332
  792.8 19.4 %psum.68 = f32[288]{0:T(512)S(1)} all-reduce(f32[288]{0:T(512)S(1)} %fusion.35), channel_id=1, replica_groups=mesh['dp'=4,'tensor'=8] {'tensor'}, use_global_device_ids=true, to_apply=%region_21.22 | all-reduce | flops 288 | bytes 2304 | tf_op jit(solution)/shard_map/psum | solution.py:335
  814.1 2.4 fusion.40
  (195 shorter events, 55.5 us)
Async XLA Ops:
  7.2 222.5 %copy-start = (bf16[64,512]{1,0:T(8,128)(2,1)S(1)}, bf16[64,512]{1,0:T(8,128)(2,1)}, u32[]{:S(2)}) copy-start(bf16[64,512]{1,0:T(8,128)(2,1)} %param.28) | copy-start | bytes 196612
  7.2 4.1 copy-start.29
  7.2 63.8 %all-gather.21.cloned.1.call-start = ((), (), s32[]{:S(2)}) async-start(), calls=%async_computation.10 | async-start | bytes 3317760 | tf_op jit(solution)/shard_map/all_gather | solution.py:95
  7.9 121.9 %all-gather.19.cloned.1.call-start = ((), (), s32[]{:S(2)}) async-start(), calls=%async_computation.9 | async-start | bytes 3317760 | tf_op jit(solution)/shard_map/all_gather | solution.py:95
  8.7 11.6 %copy-start.30 = (bf16[1152,64]{0,1:T(8,128)(2,1)S(1)}, bf16[1152,64]{0,1:T(8,128)(2,1)}, u32[]{:S(2)}) copy-start(bf16[1152,64]{0,1:T(8,128)(2,1)} %param.27) | copy-start | bytes 442372
  8.7 145.4 %all-gather.13.cloned.1.call-start = ((), (), s32[]{:S(2)}) async-start(), calls=%async_computation.4 | async-start | bytes 2949120 | tf_op jit(solution)/shard_map/all_gather | solution.py:191
  9.4 170.2 %all-gather.11.cloned.1.call-start = ((), (), s32[]{:S(2)}) async-start(), calls=%async_computation.3 | async-start | bytes 2949120 | tf_op jit(solution)/shard_map/all_gather | solution.py:192
  10.0 18.0 %copy-start.40 = (s32[3]{0:T(128)S(1)}, s32[3]{0:T(128)}, u32[]{:S(2)}) copy-start(s32[3]{0:T(128)} %param.18) | copy-start | bytes 40
  10.0 208.5 %all-gather.15.cloned.1.call-start = ((), (), s32[]{:S(2)}) async-start(), calls=%async_computation.5 | async-start | bytes 5898240 | tf_op jit(solution)/shard_map/all_gather | solution.py:190
  10.6 246.8 %all-gather.17.cloned.1.call-start = ((), (), s32[]{:S(2)}) async-start(), calls=%async_computation.6 | async-start | bytes 5898240 | tf_op jit(solution)/shard_map/all_gather | solution.py:193
  11.2 336.0 %reduce-scatter.12.cloned.1.call-start = ((), (), s32[]{:S(2)}) async-start(), calls=%async_computation.13 | async-start | bytes 3981312
  28.1 48.3 %copy-start.3 = (bf16[4608,128]{0,1:T(8,128)(2,1)}, bf16[4608,128]{0,1:T(8,128)(2,1)S(1)}, u32[]{:S(2)}) copy-start(bf16[4608,128]{0,1:T(8,128)(2,1)S(1)} %constant_dynamic-update-slice_fusion) | copy-start | bytes 3538948
  29.8 203.0 %copy-start.12 = (f32[96,64]{1,0:T(8,128)}, f32[96,64]{1,0:T(8,128)S(1)}, u32[]{:S(2)}) copy-start(f32[96,64]{1,0:T(8,128)S(1)} %get-tuple-element.50) | copy-start | bytes 73732
  135.2 12.9 %copy-start.36 = (f32[4608]{0:T(1024)S(1)}, f32[4608]{0:T(1024)}, u32[]{:S(2)}) copy-start(f32[4608]{0:T(1024)} %param.20) | copy-start | bytes 55300
  143.0 4.1 copy-start.2
  147.1 2.5 copy-start.1
  148.1 4.9 copy-start.37
  183.6 1.6 copy-start.4
  232.7 3.0 copy-start.25
  232.7 3.0 copy-start.26
  232.8 3.0 copy-start.31
  267.6 2.8 copy-start.34
  267.6 4.6 copy-start.15
  267.6 4.7 copy-start.14
  267.6 162.2 %reduce-scatter.10.cloned.1.call-start = ((), (), s32[]{:S(2)}) async-start(), calls=%async_computation.12 | async-start | bytes 3981312
  272.2 2.9 copy-start.16
  272.2 2.6 copy-start.32
  272.3 1.7 copy-start.19
  272.3 3.9 copy-start.20
  286.5 166.0 %copy-start.6 = (bf16[288,576]{1,0:T(8,128)(2,1)S(1)}, bf16[288,576]{1,0:T(8,128)(2,1)}, u32[]{:S(2)}) copy-start(bf16[288,576]{1,0:T(8,128)(2,1)} %param.17) | copy-start | bytes 995332
  286.5 287.9 %all-gather.23.cloned.1.call-start = ((), (), s32[]{:S(2)}) async-start(), calls=%async_computation.11 | async-start | bytes 3317760 | tf_op jit(solution)/shard_map/all_gather | solution.py:253
  519.0 110.6 %reduce-scatter.8.cloned.1.call-start = ((), (), s32[]{:S(2)}) async-start(), calls=%async_computation.7 | async-start | bytes 1474560 | tf_op jit(solution)/shard_map/reduce_scatter | solution.py:315
  584.4 8.5 %copy-start.33 = (pred[3,96,96]{1,2,0:T(8,128)(4,1)S(1)}, pred[3,96,96]{1,2,0:T(8,128)(4,1)}, u32[]{:S(2)}) copy-start(pred[3,96,96]{1,2,0:T(8,128)(4,1)} %broadcast_and_fusion) | copy-start | bytes 82948
  584.4 8.5 %copy-start.45 = (f32[3,2,2,96]{3,2,1,0:T(2,128)S(1)}, f32[3,2,2,96]{3,2,1,0:T(2,128)}, u32[]{:S(2)}) copy-start(f32[3,2,2,96]{3,2,1,0:T(2,128)} %copy-done.44) | copy-start | bytes 13828
  595.0 4.8 copy-start.28
  595.0 5.6 copy-start.35
  595.0 5.8 copy-start.13
  595.0 5.8 copy-start.17
  605.1 2.6 copy-start.18
  605.1 58.9 %all-reduce.5.cloned.1.call-start = ((), (), s32[]{:S(2)}) async-start(), calls=%async_computation.8 | async-start | bytes 131072 | tf_op jit(solution)/shard_map/psum | solution.py:290
  609.0 4.3 copy-start.8
  609.0 182.5 %all-reduce.7.cloned.1.call-start = ((), (), s32[]{:S(2)}) async-start(), calls=%async_computation.14 | async-start | bytes 5898240 | tf_op jit(solution)/shard_map/psum | solution.py:332
  613.3 1.7 copy-start.9
  613.3 1.7 copy-start.11
  618.7 11.6 %copy-start.42 = (f32[6,1]{0,1:T(1,128)S(1)}, f32[6,1]{0,1:T(1,128)}, u32[]{:S(2)}) copy-start(f32[6,1]{0,1:T(1,128)} %get-tuple-element.17) | copy-start | bytes 76
  618.7 172.8 %copy-start.7 = (bf16[288,576]{1,0:T(8,128)(2,1)S(1)}, bf16[288,576]{1,0:T(8,128)(2,1)}, u32[]{:S(2)}) copy-start(bf16[288,576]{1,0:T(8,128)(2,1)} %param.16) | copy-start | bytes 995332
  618.7 195.4 %copy-start.38 = (f32[288]{0:T(512)S(1)}, f32[288]{0:T(512)}, u32[]{:S(2)}) copy-start(f32[288]{0:T(512)} %copy-done.37) | copy-start | bytes 3460
  618.7 195.4 %copy-start.39 = (f32[288]{0:T(512)S(1)}, f32[288]{0:T(512)}, u32[]{:S(2)}) copy-start(f32[288]{0:T(512)} %get-tuple-element.44) | copy-start | bytes 3460
  (10 other events, 10.3 us)
Sparse Core Ops, SparseCore 0:
  10.2 60.8 all-gather.20
  73.2 56.5 all-gather.18
  131.4 22.6 all-gather.12
  155.5 24.0 all-gather.10
  181.0 37.4 all-gather.14
  219.9 37.4 all-gather.16
  267.7 79.4 reduce-scatter.11
  350.8 79.0 reduce-scatter.9
  519.1 55.2 all-gather.22
  605.2 24.2 reduce-scatter.7
  632.4 31.5 all-reduce.4
  667.5 123.9 all-reduce.6
where the time goes:
time: 829 us; the launch traced here: 824 us
  waiting for transfers between devices  514 us (62%)
  blocking collectives  125 us (15%)
  matrix products  69.4 us (8%)
  local copies, waits for them, and re-layouts  68.9 us (8%)
  other arithmetic  30.4 us (4%)
  between operations  15.1 us (2%)
    unnamed x14, waiting for transfers between devices  144 us
    psum x1, waiting for transfers between devices, body(): lax.psum(input_terms.astype(jnp.bfloat16), 'tensor').astype(jnp.float32)  126 us
    all_gather x2, waiting for transfers between devices, normalize(): whole_rows = lax.all_gather(hidden, 'tensor', axis=1, tiled=True)  87.5 us
    all_gather x1, waiting for transfers between devices, body(): lax.all_gather(grad_summed.astype(jnp.bfloat16), 'tensor', axis=1, tiled=...  55.1 us
    psum x1, blocking collectives, body(): scores = lax.psum(placed, ('dp', 'tensor'))  36.8 us
    all_gather x1, waiting for transfers between devices, body(): lax.all_gather(w_query, 'dp', axis=0, tiled=True)  32.4 us
    convert_element_type x4, local copies, waits for them, and re-layouts, normalize(): wide_rows = whole_rows.astype(jnp.float32)  25.6 us
    unnamed x98, local copies, waits for them, and re-layouts  24.7 us
  transfers between devices with their start and end apart: 12, of which 12 were waited for; matrix products, arithmetic and copies ran while one was open for 13% of the time, Pallas kernels for 0%

commit v1 on v0

--- a/solution.py
+++ b/solution.py
@@ -92,7 +92,12 @@
 
 
 def normalize(hidden, pre_gain):
-    whole_rows = lax.all_gather(hidden, "tensor", axis=1, tiled=True)
+    queue = []
+    for _ in range(lax.axis_size("tensor")):
+        queue.append(hidden)
+    arr_out = jnp.stack(queue, axis=0)
+    a_next = lax.all_to_all(arr_out, axis_name="tensor", split_axis=0, concat_axis=0)
+    whole_rows = jnp.concatenate(a_next, axis=1)
     wide_rows = whole_rows.astype(jnp.float32)
     pre_scale = lax.rsqrt(
         jnp.sum(wide_rows * wide_rows, axis=1, keepdims=True) / pre_gain.shape[0] + NORM_EPS

time: 829 us -> 827 us (level)
  waiting for transfers between devices: 514 us -> 388 us
  blocking collectives: 125 us -> 203 us
  local copies, waits for them, and re-layouts: 68.9 us -> 97.8 us
  other arithmetic: 30.4 us -> 39.8 us
    all_gather x2 -> x0, waiting for transfers between devices: 87.5 us -> none  [normalize(): whole_rows = lax.all_gather(hidden, 'tensor', axis=1, tiled=True)]
    all_to_all x0 -> x1, blocking collectives: none -> 74.4 us  [normalize(): lax.all_to_all(arr_out, axis_name='tensor', split_axis=0, concat_axis=0)]
    all_gather x1, waiting for transfers between devices: 32.4 us -> 0.02 us  [body(): lax.all_gather(w_query, 'dp', axis=0, tiled=True)]
    all_to_all x0 -> x1, waiting for transfers between devices: none -> 31 us  [normalize(): lax.all_to_all(arr_out, axis_name='tensor', split_axis=0, concat_axis=0)]
    all_gather x1, waiting for transfers between devices: 18.4 us -> 0.01 us  [body(): lax.all_gather(w_out, 'dp', axis=0, tiled=True)]
    all_gather x1, waiting for transfers between devices: 17.6 us -> 0.01 us  [body(): lax.all_gather(value_projection, 'dp', axis=0, tiled=True)]
    dot_general x0 -> x3, local copies, waits for them, and re-layouts: none -> 15.5 us  [the longest x1 6.74 us: attention_layer(): query_rows = jnp.dot(normed, w_query, preferred_element_type=jnp.float32)]
    convert_element_type x0 -> x3, local copies, waits for them, and re-layouts: none -> 14.4 us  [normalize(): normed = (wide_rows * pre_scale * pre_gain).astype(jnp.bfloat16)]
  transfers between devices with their start and end apart: 12 -> 11, of which waited for: 12 -> 7; matrix products, arithmetic and copies ran while one was open for 13% -> 16% of each run, Pallas kernels for 0% -> 0%
where the time goes in v1:
time: 827 us; the launch traced here: 815 us
  waiting for transfers between devices  388 us (47%)
  blocking collectives  203 us (25%)
  local copies, waits for them, and re-layouts  97.8 us (12%)
  matrix products  67.4 us (8%)
  other arithmetic  39.8 us (5%)
  between operations  15 us (2%)
    unnamed x12, waiting for transfers between devices  143 us
    psum x1, waiting for transfers between devices, body(): lax.psum(input_terms.astype(jnp.bfloat16), 'tensor').astype(jnp.float32)  126 us
    all_to_all x1, blocking collectives, normalize(): lax.all_to_all(arr_out, axis_name='tensor', split_axis=0, concat_axis=0)  74.4 us
    all_gather x1, waiting for transfers between devices, body(): lax.all_gather(grad_summed.astype(jnp.bfloat16), 'tensor', axis=1, tiled=...  55.6 us
    psum x1, blocking collectives, body(): scores = lax.psum(placed, ('dp', 'tensor'))  37 us
    all_to_all x1, waiting for transfers between devices, normalize(): lax.all_to_all(arr_out, axis_name='tensor', split_axis=0, concat_axis=0)  31 us
    unnamed x90, local copies, waits for them, and re-layouts  24.2 us
    psum x1, waiting for transfers between devices, body(): lax.psum(query_adapter_term.astype(jnp.bfloat16), 'dp').astype(jnp.float32)  22.5 us
  transfers between devices with their start and end apart: 11, of which 7 were waited for; matrix products, arithmetic and copies ran while one was open for 16% of the time, Pallas kernels for 0%

profile of v1, /device:TPU:0, one launch (start us, length us, event | category | flops | bytes accessed | tf_op | source)
XLA Modules:
  0.0 815.0 jit_solution(5075740816694369988)
XLA Ops:
  10.6 74.4 %all_to_all.10 = bf16[8,288,576]{2,1,0:T(8,128)(2,1)} all-to-all(bf16[8,288,576]{2,1,0:T(8,128)(2,1)S(1)} %stack.13), channel_id=1, replica_groups=mesh['dp'=4,'tensor'=8] {'tensor'}, dimensions={0} | all-to-all | bytes 5308416 | tf_op jit(solution)/shard_map/all_to_all | solution.py:99
  86.9 3.8 all-to-all-start
  91.4 11.4 %all_gather.22 = bf16[4608,64]{0,1:T(8,128)(2,1)S(1)} all-gather(bf16[1152,64]{0,1:T(8,128)(2,1)} %param.26), channel_id=1, replica_groups=mesh['dp'=4,'tensor'=8] {'dp'}, dimensions={0}, use_global_device_ids=true | all-gather | bytes 737280 | tf_op jit(solution)/shard_map/all_gather | solution.py:199
  102.8 7.8 all_gather.23
  114.0 4.4 copy.80
  118.4 4.3 copy.73
  122.8 2.6 fusion.2
  125.4 31.0 %all-to-all-done = bf16[8,288,576]{2,1,0:T(8,128)(2,1)S(1)} async-done(((bf16[8,288,576]{2,1,0:T(8,128)(2,1)}), bf16[8,288,576]{2,1,0:T(8,128)(2,1)S(1)}, u32[]{:S(2)}, u32[]{:S(2)}) %all-to-all-start) | async-done | bytes 2654240 | tf_op jit(solution)/shard_map/all_to_all | solution.py:99
  158.2 3.4 fusion.9
  161.6 2.6 copy.79
  164.2 5.6 reshape.358
  170.2 5.9 copy.71
  176.1 7.3 reshape.351
  183.4 2.6 copy.72
  186.0 6.2 reshape.354
  192.3 2.7 fusion.12
  197.4 3.2 multiply_convert_fusion
  200.6 2.1 convolution_convert_fusion.6
  202.7 6.7 copy.81
  209.4 3.9 fusion.160
  218.1 4.3 fusion.10
  225.0 4.6 fusion.31
  231.7 5.5 convolution_convert_fusion
  237.2 4.7 copy.113
  241.9 2.5 fusion.159
  248.7 5.6 convolution_convert_fusion.1
  254.3 4.7 copy.111
  261.1 59.4 %reduce-scatter.12.cloned.1.call-done = bf16[576,288]{1,0:T(8,128)(2,1)} async-done(((bf16[4608,288]{1,0:T(8,128)(2,1)}), bf16[576,288]{1,0:T(8,128)(2,1)}) %reduce-scatter.12.cloned.1.call-update) | async-done | bytes 331792
  322.5 80.6 %reduce-scatter.10.cloned.1.call-done = bf16[576,288]{1,0:T(8,128)(2,1)} async-done(((bf16[4608,288]{1,0:T(8,128)(2,1)}), bf16[576,288]{1,0:T(8,128)(2,1)}) %reduce-scatter.10.cloned.1.call-update) | async-done | bytes 331792
  406.8 20.7 %all-reduce = (f32[288]{0:T(512)}, f32[288]{0:T(512)}) all-reduce(f32[288]{0:T(512)} %fusion.69, f32[288]{0:T(512)} %fusion.56), channel_id=1, replica_groups=mesh['dp'=4,'tensor'=8] {'tensor'}, use_global_device_ids=true, to_apply=%region_4.5 | all-reduce | flops 576 | bytes 4608 | tf_op jit(solution)/shard_map/psum | solution.py:151
  429.3 3.2 fusion.67
  439.7 37.0 %psum.65 = f32[2,12]{1,0:T(2,128)} all-reduce(f32[2,12]{1,0:T(2,128)} %dynamic_update_slice.3), channel_id=1, replica_groups=mesh['dp'=4,'tensor'=8] {'dp','tensor'}, use_global_device_ids=true, to_apply=%region_14.15 | all-reduce | flops 24 | bytes 192 | tf_op jit(solution)/shard_map/psum | solution.py:231
  486.8 21.8 %psum.66 = f32[288]{0:T(512)} all-reduce(f32[288]{0:T(512)} %fusion.62), channel_id=1, replica_groups=mesh['dp'=4,'tensor'=8] {'tensor'}, use_global_device_ids=true, to_apply=%region_17.18 | all-reduce | flops 288 | bytes 2304 | tf_op jit(solution)/shard_map/psum | solution.py:253
  510.8 55.6 %all-gather.15.cloned.1.call-done = bf16[8,576,288]{1,2,0:T(8,128)(2,1)} async-done(((bf16[1,576,288]{1,2,0:T(8,128)(2,1)}), bf16[8,576,288]{1,2,0:T(8,128)(2,1)}) %all-gather.15.cloned.1.call-update) | async-done | bytes 2654224 | tf_op jit(solution)/shard_map/all_gather | solution.py:258
  566.4 4.4 copy.86
  570.8 5.6 reshape.353
  576.4 5.4 convolution_convert_fusion.3
  587.0 3.3 fusion.51
  594.3 2.2 convolution_convert_fusion.2
  596.6 2.5 convolution_bitcast_fusion.2
  600.7 4.3 fusion.82
  607.7 3.7 fusion.1
  611.4 9.6 %reduce-scatter.8.cloned.1.call-done = bf16[1152,128]{1,0:T(8,128)(2,1)} async-done(((bf16[4608,128]{1,0:T(8,128)(2,1)}), bf16[1152,128]{1,0:T(8,128)(2,1)}) %reduce-scatter.8.cloned.1.call-update) | async-done | bytes 294928 | tf_op jit(solution)/shard_map/reduce_scatter | solution.py:320
  622.0 10.3 %psum.71 = bf16[64,256]{1,0:T(8,128)(2,1)S(1)} all-reduce(bf16[64,256]{1,0:T(8,128)(2,1)S(1)} %fusion.47), channel_id=1, replica_groups=mesh['dp'=4,'tensor'=8] {'dp'}, use_global_device_ids=true, to_apply=%region_25.26 | all-reduce | flops 16384 | bytes 65536 | tf_op jit(solution)/shard_map/psum | solution.py:296
  632.9 22.5 %all-reduce.5.cloned.1.call-done = bf16[64,512]{1,0:T(8,128)(2,1)} async-done(((bf16[64,512]{1,0:T(8,128)(2,1)}), bf16[64,512]{1,0:T(8,128)(2,1)}) %all-reduce.5.cloned.1.call-update) | async-done | bytes 65552 | tf_op jit(solution)/shard_map/psum | solution.py:295
  657.0 126.0 %all-reduce.7.cloned.1.call-done = (bf16[288,4608]{1,0:T(8,128)(2,1)}, bf16[1152,128]{1,0:T(8,128)(2,1)}) async-done(((bf16[288,4608]{1,0:T(8,128)(2,1)}, bf16[1152,128]{1,0:T(8,128)(2,1)}), (bf16[288,4608]{1,0:T(8,128)(2,1)}, bf16[1152,128]{1,0:T(8,128)(2,1)})) %all-reduce.7.cloned.1.call-update) | async-done | bytes 2949136 | tf_op jit(solution)/shard_map/psum | solution.py:337
  784.3 19.4 %psum.68 = f32[288]{0:T(512)S(1)} all-reduce(f32[288]{0:T(512)S(1)} %fusion.59), channel_id=1, replica_groups=mesh['dp'=4,'tensor'=8] {'tensor'}, use_global_device_ids=true, to_apply=%region_21.22 | all-reduce | flops 288 | bytes 2304 | tf_op jit(solution)/shard_map/psum | solution.py:340
  805.5 2.4 fusion.64
  (184 shorter events, 76.0 us)
Async XLA Ops:
  7.2 206.1 %copy-start = (bf16[64,512]{1,0:T(8,128)(2,1)S(1)}, bf16[64,512]{1,0:T(8,128)(2,1)}, u32[]{:S(2)}) copy-start(bf16[64,512]{1,0:T(8,128)(2,1)} %param.28) | copy-start | bytes 196612
  7.2 106.8 %all-gather.7.cloned.1.call-start = ((), (), s32[]{:S(2)}) async-start(), calls=%async_computation.5 | async-start | bytes 2949120 | tf_op jit(solution)/shard_map/all_gather | solution.py:197
  7.9 110.5 %all-gather.9.cloned.1.call-start = ((), (), s32[]{:S(2)}) async-start(), calls=%async_computation.6 | async-start | bytes 2949120 | tf_op jit(solution)/shard_map/all_gather | solution.py:196
  8.7 194.0 %all-gather.11.cloned.1.call-start = ((), (), s32[]{:S(2)}) async-start(), calls=%async_computation.7 | async-start | bytes 5898240 | tf_op jit(solution)/shard_map/all_gather | solution.py:195
  10.6 74.4 %copy-start.5 = (bf16[288,576]{1,0:T(8,128)(2,1)S(1)}, bf16[288,576]{1,0:T(8,128)(2,1)}, u32[]{:S(2)}) copy-start(bf16[288,576]{1,0:T(8,128)(2,1)} %param.16) | copy-start | bytes 995332
  86.9 4.4 copy-start.25
  86.9 69.5 %all-to-all-start = ((bf16[8,288,576]{2,1,0:T(8,128)(2,1)}), bf16[8,288,576]{2,1,0:T(8,128)(2,1)S(1)}, u32[]{:S(2)}, u32[]{:S(2)}) async-start(bf16[8,288,576]{2,1,0:T(8,128)(2,1)} %stack.12), calls=%async_computation | async-start | bytes 5898240 | tf_op jit(solution)/shard_map/all_to_all | solution.py:99
  90.7 20.0 %copy-start.36 = (s32[3]{0:T(128)S(1)}, s32[3]{0:T(128)}, u32[]{:S(2)}) copy-start(s32[3]{0:T(128)} %param.18) | copy-start | bytes 40
  90.7 141.0 %all-gather.13.cloned.1.call-start = ((), (), s32[]{:S(2)}) async-start(), calls=%async_computation.8 | async-start | bytes 5898240 | tf_op jit(solution)/shard_map/all_gather | solution.py:198
  91.2 229.3 %reduce-scatter.12.cloned.1.call-start = ((), (), s32[]{:S(2)}) async-start(), calls=%async_computation.13 | async-start | bytes 3981312
  112.3 84.0 %copy-start.15 = (f32[96,64]{1,0:T(8,128)}, f32[96,64]{1,0:T(8,128)S(1)}, u32[]{:S(2)}) copy-start(f32[96,64]{1,0:T(8,128)S(1)} %get-tuple-element.45) | copy-start | bytes 73732
  112.3 110.1 %copy-start.12 = (f32[96,64]{1,0:T(8,128)}, f32[96,64]{1,0:T(8,128)S(1)}, u32[]{:S(2)}) copy-start(f32[96,64]{1,0:T(8,128)S(1)} %get-tuple-element.46) | copy-start | bytes 73732
  156.4 1.8 copy-start.1
  157.7 39.7 %copy-start.32 = (f32[288]{0:T(512)}, f32[288]{0:T(512)S(1)}, u32[]{:S(2)}) copy-start(f32[288]{0:T(512)S(1)} %get-tuple-element.41) | copy-start | bytes 3460
  176.1 7.3 copy-start.2
  186.0 6.2 copy-start.7
  192.2 2.7 copy-start.8
  192.2 3.2 copy-start.9
  218.0 4.4 copy-start.16
  222.4 1.3 copy-start.22
  222.4 1.3 copy-start.23
  222.4 1.3 copy-start.26
  241.9 2.6 copy-start.30
  241.9 2.9 copy-start.27
  241.9 161.2 %reduce-scatter.10.cloned.1.call-start = ((), (), s32[]{:S(2)}) async-start(), calls=%async_computation.12 | async-start | bytes 3981312
  244.8 1.8 copy-start.14
  246.5 0.8 copy-start.39
  246.5 7.8 copy-start.40
  259.0 307.3 %all-gather.15.cloned.1.call-start = ((), (), s32[]{:S(2)}) async-start(), calls=%async_computation.11 | async-start | bytes 3317760 | tf_op jit(solution)/shard_map/all_gather | solution.py:258
  510.7 110.3 %reduce-scatter.8.cloned.1.call-start = ((), (), s32[]{:S(2)}) async-start(), calls=%async_computation.9 | async-start | bytes 1474560 | tf_op jit(solution)/shard_map/reduce_scatter | solution.py:320
  576.4 8.5 %copy-start.28 = (pred[3,96,96]{1,2,0:T(8,128)(4,1)S(1)}, pred[3,96,96]{1,2,0:T(8,128)(4,1)}, u32[]{:S(2)}) copy-start(pred[3,96,96]{1,2,0:T(8,128)(4,1)} %broadcast_and_fusion) | copy-start | bytes 82948
  576.4 8.5 %copy-start.41 = (f32[3,2,2,96]{3,2,1,0:T(2,128)S(1)}, f32[3,2,2,96]{3,2,1,0:T(2,128)}, u32[]{:S(2)}) copy-start(f32[3,2,2,96]{3,2,1,0:T(2,128)} %copy-done.40) | copy-start | bytes 13828
  587.0 3.3 copy-start.13
  590.2 1.9 copy-start.24
  590.2 2.7 copy-start.31
  596.5 2.6 copy-start.17
  596.6 58.9 %all-reduce.5.cloned.1.call-start = ((), (), s32[]{:S(2)}) async-start(), calls=%async_computation.10 | async-start | bytes 131072 | tf_op jit(solution)/shard_map/psum | solution.py:295
  600.4 4.6 copy-start.4
  600.4 182.5 %all-reduce.7.cloned.1.call-start = ((), (), s32[]{:S(2)}) async-start(), calls=%async_computation.14 | async-start | bytes 5898240 | tf_op jit(solution)/shard_map/psum | solution.py:337
  605.1 1.7 copy-start.3
  605.1 1.7 copy-start.11
  606.7 0.9 copy-start.19
  606.7 0.9 copy-start.21
  611.3 9.8 %copy-start.38 = (f32[6,1]{0,1:T(1,128)S(1)}, f32[6,1]{0,1:T(1,128)}, u32[]{:S(2)}) copy-start(f32[6,1]{0,1:T(1,128)} %get-tuple-element.17) | copy-start | bytes 76
  611.3 194.2 %copy-start.6 = (bf16[288,576]{1,0:T(8,128)(2,1)S(1)}, bf16[288,576]{1,0:T(8,128)(2,1)}, u32[]{:S(2)}) copy-start(bf16[288,576]{1,0:T(8,128)(2,1)} %param.17) | copy-start | bytes 995332
  611.3 194.2 %copy-start.29 = (f32[288]{0:T(512)S(1)}, f32[288]{0:T(512)}, u32[]{:S(2)}) copy-start(f32[288]{0:T(512)} %mul.780) | copy-start | bytes 3460
  611.3 194.2 %copy-start.33 = (f32[288]{0:T(512)S(1)}, f32[288]{0:T(512)}, u32[]{:S(2)}) copy-start(f32[288]{0:T(512)} %copy-done.32) | copy-start | bytes 3460
  611.3 194.2 %copy-start.35 = (f32[288]{0:T(512)S(1)}, f32[288]{0:T(512)}, u32[]{:S(2)}) copy-start(f32[288]{0:T(512)} %get-tuple-element.40) | copy-start | bytes 3460
  (5 other events, 3.1 us)
Sparse Core Ops, SparseCore 0:
  9.5 26.7 all-gather.6
  37.9 24.0 all-gather.8
  63.6 40.5 all-gather.10
  105.6 37.4 all-gather.12
  242.0 78.5 reduce-scatter.11
  324.0 79.0 reduce-scatter.9
  510.8 55.4 all-gather.14
  596.7 24.2 reduce-scatter.7
  623.9 31.5 all-reduce.4
  659.0 123.9 all-reduce.6
